TPU v7x, 32 devices: a 4x4x1 block of a 4x4x8 slice. The times are simulated.
32 devices in a mesh: dp: 1 (over z), tp: 4 (over y), sp: 8 (over x, core).
Axes of the slice: x: 4, y: 4, z: 1, core: 2. Of those that a mesh axis runs over, the one named last changes fastest.
The devices are a block of a 4x4x8 slice.
Arguments:
- hidden: bfloat16 [256, 4096], P('dp')
- norm_w: bfloat16 [4096], replicated
- w_q: bfloat16 [4096, 12288], P(None, 'tp')
- b_q: bfloat16 [12288], P('tp')
- w_k: bfloat16 [4096, 1024], P(None, 'tp')
- b_k: bfloat16 [1024], P('tp')
- w_v: bfloat16 [4096, 1024], P(None, 'tp')
- b_v: bfloat16 [1024], P('tp')
- w_o: bfloat16 [12288, 4096], P('tp')
- k_cache: bfloat16 [256, 1024, 8, 128], P('dp', 'sp', 'tp')
- v_cache: bfloat16 [256, 1024, 8, 128], P('dp', 'sp', 'tp')
- positions: int32 [256], P('dp')
- seq_lens: int32 [256], P('dp')
Outputs:
- output 1: bfloat16 [256, 4096], P('dp')
- output 2: bfloat16 [256, 8, 128], P('dp', 'tp')
- output 3: bfloat16 [256, 8, 128], P('dp', 'tp')
All inputs are finite; a program needn't handle non-finite values.
Results may differ from a plain program's by a relative error of at most 0.00743964.
Values sent between devices are 32-bit elements.
A program may use at most 768 MiB of HBM per device.

v0:
```python
import jax
import jax.numpy as jnp
from jax import lax
from jax.sharding import PartitionSpec as P

RMS_EPS = 1.5625e-7
ROPE_BASE = 10000.0
NEG_BIG = -1e30


def rms_norm(x_rows, norm_w):
    x_f32 = x_rows.astype(jnp.float32)
    mean_sq = jnp.mean(x_f32 * x_f32, axis=-1, keepdims=True)
    return (x_f32 * lax.rsqrt(mean_sq + RMS_EPS) * norm_w.astype(jnp.float32)).astype(jnp.bfloat16)


def apply_rotary(heads_in, positions):
    rot_dim = heads_in.shape[-1] // 2
    half_rot = rot_dim // 2
    inv_freq = ROPE_BASE ** (-2.0 * jnp.arange(half_rot, dtype=jnp.float32) / rot_dim)
    angles = positions.astype(jnp.float32)[:, None, None] * inv_freq
    cos_t = jnp.cos(angles)
    sin_t = jnp.sin(angles)
    rot_pairs = heads_in[..., :rot_dim].astype(jnp.float32).reshape(heads_in.shape[:-1] + (half_rot, 2))
    even_part = rot_pairs[..., 0]
    odd_part = rot_pairs[..., 1]
    rotated = jnp.stack([even_part * cos_t - odd_part * sin_t, even_part * sin_t + odd_part * cos_t], axis=-1)
    rotated = rotated.reshape(heads_in.shape[:-1] + (rot_dim,)).astype(jnp.bfloat16)
    return jnp.concatenate([rotated, heads_in[..., rot_dim:]], axis=-1)


def project(normed, weight, bias_vec):
    return (jnp.dot(normed, weight, preferred_element_type=jnp.float32) + bias_vec.astype(jnp.float32)).astype(jnp.bfloat16)


def local_partials(q_grp, k_rot, v_new, k_loc, v_loc, seq_lens, shard_idx):
    s_dev = k_loc.shape[1]
    attn_scale = q_grp.shape[-1] ** -0.5
    cache_pos = shard_idx * s_dev + jnp.arange(s_dev, dtype=jnp.int32)
    valid_mask = (cache_pos[None, :] < seq_lens[:, None])[:, None, None, :]
    s_cache = jnp.einsum('bgqd,bsgd->bgqs', q_grp, k_loc, preferred_element_type=jnp.float32) * attn_scale
    s_cache = jnp.where(valid_mask, s_cache, NEG_BIG)
    is_first = shard_idx == 0
    s_new = jnp.einsum('bgqd,bgd->bgq', q_grp, k_rot, preferred_element_type=jnp.float32) * attn_scale
    s_new = jnp.where(is_first, s_new, NEG_BIG)
    m_loc = jnp.maximum(jnp.max(s_cache, axis=-1), s_new)
    p_cache = jnp.where(valid_mask, jnp.exp(s_cache - m_loc[..., None]), 0.0)
    p_new = jnp.where(is_first, jnp.exp(s_new - m_loc), 0.0)
    l_loc = jnp.sum(p_cache, axis=-1) + p_new
    o_loc = jnp.einsum('bgqs,bsgd->bgqd', p_cache.astype(jnp.bfloat16), v_loc, preferred_element_type=jnp.float32)
    o_loc = o_loc + p_new[..., None] * v_new.astype(jnp.float32)[:, :, None, :]
    return m_loc, l_loc, o_loc


def solution(mesh):
    def device_step(hidden, norm_w, w_q, b_q, w_k, b_k, w_v, b_v, w_o, k_cache, v_cache, positions, seq_lens):
        n_rows = hidden.shape[0]
        groups_dev, head_dim = k_cache.shape[2], k_cache.shape[3]
        heads_dev = w_q.shape[1] // head_dim
        per_group = heads_dev // groups_dev
        normed = rms_norm(hidden, norm_w)
        q_rot = apply_rotary(project(normed, w_q, b_q).reshape(n_rows, heads_dev, head_dim), positions)
        k_rot = apply_rotary(project(normed, w_k, b_k).reshape(n_rows, groups_dev, head_dim), positions)
        v_new = project(normed, w_v, b_v).reshape(n_rows, groups_dev, head_dim)
        q_grp = q_rot.reshape(n_rows, groups_dev, per_group, head_dim)
        m_loc, l_loc, o_loc = local_partials(q_grp, k_rot, v_new, k_cache, v_cache, seq_lens, lax.axis_index('sp'))
        m_all = lax.pmax(m_loc, 'sp')
        factor = jnp.exp(m_loc - m_all)
        l_all, o_all = lax.psum((l_loc * factor, o_loc * factor[..., None]), 'sp')
        attn_rows = (o_all / l_all[..., None]).astype(jnp.bfloat16).reshape(n_rows, heads_dev * head_dim)
        proj_sum = lax.psum(jnp.dot(attn_rows, w_o, preferred_element_type=jnp.float32), 'tp')
        y_out = (hidden.astype(jnp.float32) + proj_sum).astype(jnp.bfloat16)
        return y_out, k_rot, v_new

    col_spec = P(None, 'tp')
    vec_spec = P('tp')
    cache_spec = P('dp', 'sp', 'tp', None)
    group_spec = P('dp', 'tp', None)
    in_specs = (P('dp', None), P(None), col_spec, vec_spec, col_spec, vec_spec, col_spec, vec_spec,
                P('tp', None), cache_spec, cache_spec, P('dp'), P('dp'))
    out_specs = (P('dp', None), group_spec, group_spec)
    return jax.shard_map(device_step, mesh=mesh, in_specs=in_specs, out_specs=out_specs, check_vma=False)
```

profile of v0, /device:TPU:97, one launch (start us, length us, event | category | flops | bytes accessed | tf_op | source)
XLA Modules:
  0.0 292.5 jit_solution(13486732843947365953)
XLA Ops:
  7.3 0.8 convert_element_type.65
  8.1 0.7 convert_element_type.69
  8.7 0.7 convert_element_type.63
  9.4 2.2 fusion.4
  11.7 0.7 convert_element_type.61
  12.4 0.7 convert_element_type.59
  13.1 2.8 fusion.26
  16.1 1.2 fusion.27
  18.1 0.9 copy.60
  19.0 12.0 %fusion.25 = bf16[32,8,24,128]{3,1,2,0:T(8,128)(2,1)S(1)} fusion(f32[3072]{0:T(1024)S(1)} %convert_element_type.61, bf16[4096,3072]{1,0:T(8,128)(2,1)} %param.15, bf16[256,4096]{1,0:T(8,128)(2,1)S(1)} %copy-done.4, f32[4096]{0:T(1024)S(1)} %convert_element_type.59, f32[256]{0:T(256)S(1)} %add_rsqrt_fusion), kind=kOutput, calls=%fused_computation.29 | convolution fusion | flops 6448218112 | bytes 28865536 | tf_op jit(solution)/shard_map/dot_general | solution.py:33
  31.0 0.3 copy.65
  31.3 2.4 fusion.35
  33.7 2.4 copy.62
  36.3 0.3 subtract_convert_fusion
  36.5 2.4 copy.63
  39.0 1.3 pad_maximum_fusion
  40.3 2.1 copy.49
  42.5 1.3 fusion.12
  43.8 14.0 %fusion.9 = (f32[256,2,12]{2,1,0:T(2,128)S(1)}, f32[256,2,12,128]{3,2,1,0:T(8,128)}) fusion(pred[256,128]{1,0:T(8,128)(4,1)S(1)} %broadcast_compare_fusion, bf16[256,128,2,128]{3,2,1,0:T(2,128)(2,1)} %param.22, bf16[256,2,12,128]{3,0,2,1:T(8,128)(2,1)S(1)} %bitcast.24), kind=kOutput, calls=%fused_computation.17 | convolution fusion | flops 203679744 | bytes 21553152 | tf_op jit(solution)/shard_map/bgqd,bsgd->bgqs/dot_general | solution.py:41
  58.0 26.7 %pmax.7 = f32[256,2,12]{2,1,0:T(2,128)S(1)} all-reduce(f32[256,2,12]{2,1,0:T(2,128)S(1)} %fusion.28), channel_id=1, replica_groups=mesh['dp'=1,'tp'=4,'sp'=8] {'sp'}, use_global_device_ids=true, to_apply=%region_2.3 | all-reduce | flops 6144 | bytes 49152 | tf_op jit(solution)/shard_map/pmax | solution.py:67
  84.8 7.4 %fusion.10 = f32[256,2,12]{2,1,0:T(2,128)S(1)} fusion(f32[256,2,12,128]{3,2,1,0:T(8,128)} %get-tuple-element.29, f32[256,2,12]{2,1,0:T(2,128)S(1)} %fusion.28, pred[256,128]{1,0:T(8,128)(4,1)S(1)} %broadcast_compare_fusion), kind=kLoop, calls=%fused_computation.18 | loop fusion | flops 3926016 | bytes 3227648 | tf_op jit(solution)/shard_map/reduce_sum | solution.py:49
  92.2 0.5 add_multiply_fusion.1
  92.7 10.2 %add_multiply_fusion = f32[256,2,12,128]{3,2,1,0:T(8,128)} fusion(f32[256,2,12]{2,1,0:T(2,128)S(1)} %get-tuple-element.17, f32[256,2,128]{2,1,0:T(2,128)S(1)} %copy.56, f32[256,2,12]{2,1,0:T(2,128)S(1)} %get-tuple-element.16, bf16[256,128,2,128]{3,2,1,0:T(2,128)(2,1)} %param.23, f32[256,2,12,128]{3,2,1,0:T(8,128)S(1)} %copy-done.2, ...), kind=kOutput, calls=%fused_computation.12 | convolution fusion | flops 207618048 | bytes 23437312 | tf_op jit(solution)/shard_map/bgqs,bsgd->bgqd/dot_general | solution.py:50
  103.0 29.1 %psum.22 = f32[256,2,12]{2,1,0:T(2,128)S(1)} all-reduce(f32[256,2,12]{2,1,0:T(2,128)S(1)} %get-tuple-element.15), channel_id=1, replica_groups=mesh['dp'=1,'tp'=4,'sp'=8] {'sp'}, use_global_device_ids=true, to_apply=%region_5.6 | all-reduce | flops 6144 | bytes 49152 | tf_op jit(solution)/shard_map/psum | solution.py:69
  132.1 40.7 %all-reduce.3.cloned.1.call-done = f32[256,2,12,128]{3,2,1,0:T(8,128)} async-done(((f32[256,2,12,128]{3,2,1,0:T(8,128)}), f32[256,2,12,128]{3,2,1,0:T(8,128)}) %all-reduce.3.cloned.1.call-update) | async-done | bytes 3145744 | tf_op jit(solution)/shard_map/psum | solution.py:69
  172.8 2.9 divide_convert_fusion
  175.6 2.6 copy.57
  178.3 13.4 %fusion.36 = f32[256,4096]{1,0:T(8,128)} fusion(bf16[256,3072]{0,1:T(8,128)(2,1)} %bitcast.25, bf16[3072,4096]{1,0:T(8,128)(2,1)} %param.21), kind=kOutput, calls=%fused_computation.57 | convolution fusion | flops 6442450944 | bytes 30932992 | tf_op jit(solution)/shard_map/dot_general | solution.py:71
  191.7 0.8 copy.59
  192.7 0.8 copy.58
  193.5 87.5 %all-reduce.5.cloned.1.call-done = f32[256,4096]{1,0:T(8,128)} async-done(((f32[256,4096]{1,0:T(8,128)}), f32[256,4096]{1,0:T(8,128)}) %all-reduce.5.cloned.1.call-update) | async-done | bytes 4194320 | tf_op jit(solution)/shard_map/psum | solution.py:71
  280.9 4.7 %fusion.7 = bf16[256,4096]{1,0:T(8,128)(2,1)} fusion(f32[256,4096]{1,0:T(8,128)} %all-reduce.5.cloned.1.call-done, bf16[256,4096]{1,0:T(8,128)(2,1)} %param.13), kind=kLoop, calls=%fused_computation.10 | loop fusion | flops 3145728 | bytes 8388608 | tf_op jit(solution)/shard_map/convert_element_type | solution.py:72
  (37 shorter events, 2.1 us)
Async XLA Ops:
  7.2 5.9 %copy-start = (bf16[4096,256]{1,0:T(8,128)(2,1)S(1)}, bf16[4096,256]{1,0:T(8,128)(2,1)}, u32[]{:S(2)}) copy-start(bf16[4096,256]{1,0:T(8,128)(2,1)} %param.17) | copy-start | bytes 6291460
  7.2 165.6 %all-reduce.3.cloned.1.call-start = ((), (), s32[]{:S(2)}) async-start(), calls=%async_computation | async-start | bytes 8388608 | tf_op jit(solution)/shard_map/psum | solution.py:69
  9.4 6.6 %copy-start.3 = (bf16[256,4096]{1,0:T(8,128)(2,1)S(1)}, bf16[256,4096]{1,0:T(8,128)(2,1)}, u32[]{:S(2)}) copy-start(bf16[256,4096]{1,0:T(8,128)(2,1)} %param.13) | copy-start | bytes 6291460
  9.4 6.6 %copy-start.7 = (bf16[4096,256]{1,0:T(8,128)(2,1)S(1)}, bf16[4096,256]{1,0:T(8,128)(2,1)}, u32[]{:S(2)}) copy-start(bf16[4096,256]{1,0:T(8,128)(2,1)} %param.19) | copy-start | bytes 6291460
  15.8 3.2 %copy-start.4 = (bf16[256,4096]{1,0:T(8,128)(2,1)S(1)}, bf16[256,4096]{1,0:T(8,128)(2,1)}, u32[]{:S(2)}) copy-start(bf16[256,4096]{1,0:T(8,128)(2,1)} %param.13) | copy-start | bytes 6291460
  38.9 3.5 %copy-start.6 = (s32[256]{0:T(256)S(1)}, s32[256]{0:T(256)}, u32[]{:S(2)}) copy-start(s32[256]{0:T(256)} %param.25) | copy-start | bytes 3076
  38.9 3.6 %copy-start.5 = (bf16[256,2,128,1]{2,3,1,0:T(2,128)(2,1)S(1)}, bf16[256,2,128,1]{2,3,1,0:T(2,128)(2,1)}, u32[]{:S(2)}) copy-start(bf16[256,2,128,1]{2,3,1,0:T(2,128)(2,1)} %copy.60) | copy-start | bytes 393220
  84.7 8.0 %copy-start.2 = (f32[256,2,12,128]{3,2,1,0:T(8,128)S(1)}, f32[256,2,12,128]{3,2,1,0:T(8,128)}, u32[]{:S(2)}) copy-start(f32[256,2,12,128]{3,2,1,0:T(8,128)} %get-tuple-element.29) | copy-start | bytes 9437188
  103.0 178.0 %all-reduce.5.cloned.1.call-start = ((), (), s32[]{:S(2)}) async-start(), calls=%async_computation.1 | async-start | bytes 8388608 | tf_op jit(solution)/shard_map/psum | solution.py:71
  192.7 93.0 %copy-start.1 = (bf16[4096,256]{1,0:T(8,128)(2,1)S(1)}, bf16[4096,256]{1,0:T(8,128)(2,1)}, u32[]{:S(2)}) copy-start(bf16[4096,256]{1,0:T(8,128)(2,1)} %param.17) | copy-start | bytes 6291460
Sparse Core Ops, SparseCore 0:
  103.1 69.6 all-reduce.2
  191.8 89.0 all-reduce.4
where the time goes:
time: 293 us
  waiting for transfers between devices  128 us (44%)
  blocking collectives  55.8 us (19%)
  matrix products  54.7 us (19%)
  other arithmetic  24.2 us (8%)
  local copies, waits for them, and re-layouts  15.1 us (5%)
  between operations  14.4 us (5%)
    psum x1, waiting for transfers between devices, device_step(): lax.psum(jnp.dot(attn_rows, w_o, preferred_element_type=jnp.float32), 'tp')  87.5 us
    psum x1, waiting for transfers between devices, device_step(): l_all, o_all = lax.psum((l_loc * factor, o_loc * factor[..., None]), 'sp')  40.7 us
    psum x1, blocking collectives, device_step(): l_all, o_all = lax.psum((l_loc * factor, o_loc * factor[..., None]), 'sp')  29.1 us
    pmax x1, blocking collectives, device_step(): m_all = lax.pmax(m_loc, 'sp')  26.7 us
    dot_general x3, matrix products, project(): jnp.dot(normed, weight, preferred_element_type=jnp.float32)  15.9 us
    dot_general x1, matrix products, local_partials(): jnp.einsum('bgqd,bsgd->bgqs', q_grp, k_loc, preferred_element_type=jnp.fl...  14 us
    dot_general x1, matrix products, device_step(): jnp.dot(attn_rows, w_o, preferred_element_type=jnp.float32)  13.4 us
    dot_general x1, matrix products, local_partials(): jnp.einsum('bgqs,bsgd->bgqd', p_cache.astype(jnp.bfloat16), v_loc, prefer...  10.2 us
  transfers between devices with their start and end apart: 2, of which 2 were waited for; matrix products, arithmetic and copies ran while one was open for 1% of the time, Pallas kernels for 0%

commit v1 on v0

v1 whole, which is shorter than its diff:
```python
import functools

import jax
import jax.numpy as jnp
from jax import lax
from jax.experimental import pallas as pl
from jax.experimental.pallas import tpu as pltpu
from jax.sharding import PartitionSpec as P

RMS_EPS = 1.5625e-7
ROPE_BASE = 10000.0
NEG_BIG = -1e30
F32 = jnp.float32
BF16 = jnp.bfloat16
MESH = pl.DeviceIdType.MESH
HALF = 16
ML_ROWS = HALF + 1
VMEM_SPEC = pl.BlockSpec(memory_space=pltpu.VMEM)
ANY_SPEC = pl.BlockSpec(memory_space=pl.ANY)


def rope(heads, cos_t, sin_t):
    lane = lax.broadcasted_iota(jnp.int32, heads.shape, 1)
    width = heads.shape[1]
    swapped = jnp.where(lane % 2 == 0, pltpu.roll(heads, width - 1, 1), pltpu.roll(heads, 1, 1))
    rotated = (heads * cos_t + swapped * sin_t).astype(BF16).astype(F32)
    return jnp.where(lane < width // 2, rotated, heads)


def qkv_kernel(n_tiles, head_dim, hid_ref, nw_ref, cos_ref, sin_ref, wq_ref, bq_ref, wk_ref, bk_ref, wv_ref, bv_ref,
               q_ref, k_ref, v_ref, kb_ref, vb_ref, normed, wk_buf, wv_buf, sems):
    step = pl.program_id(0)
    n_rows = hid_ref.shape[0]

    def small_copies():
        return (pltpu.make_async_copy(wk_ref, wk_buf, sems.at[0]), pltpu.make_async_copy(wv_ref, wv_buf, sems.at[1]))

    @pl.when(step == 0)
    def _():
        for copy in small_copies():
            copy.start()

        def norm_rows(i, carry):
            rows = pl.ds(pl.multiple_of(i * 16, 16), 16)
            x = hid_ref[rows, :].astype(F32)
            mean_sq = jnp.mean(x * x, axis=1, keepdims=True)
            normed[rows, :] = (x * lax.rsqrt(mean_sq + RMS_EPS) * nw_ref[...]).astype(BF16)
            return carry
        lax.fori_loop(0, n_rows // 16, norm_rows, 0)

    @pl.when(step < n_tiles)
    def _():
        acc = jnp.dot(normed[...], wq_ref[...], preferred_element_type=F32) + bq_ref[0]
        acc = acc.astype(BF16).astype(F32)
        for h in range(acc.shape[1] // head_dim):
            q_ref[h * n_rows:(h + 1) * n_rows, :] = rope(acc[:, h * head_dim:(h + 1) * head_dim], cos_ref[...], sin_ref[...])

    @pl.when(step == n_tiles)
    def _():
        for copy in small_copies():
            copy.wait()
        k = (jnp.dot(normed[...], wk_buf[...], preferred_element_type=F32) + bk_ref[...]).astype(BF16).astype(F32)
        v = (jnp.dot(normed[...], wv_buf[...], preferred_element_type=F32) + bv_ref[...]).astype(BF16)
        vb_ref[...] = v
        v = v.astype(F32)
        for g in range(k.shape[1] // head_dim):
            cols = slice(g * head_dim, (g + 1) * head_dim)
            rows = slice(g * n_rows, (g + 1) * n_rows)
            rotated = rope(k[:, cols], cos_ref[...], sin_ref[...])
            k_ref[rows, :] = rotated
            kb_ref[:, cols] = rotated.astype(BF16)
            v_ref[rows, :] = v[:, cols]


def qkv_project(hidden, norm_w, cos_t, sin_t, w_q, b_q, w_k, b_k, w_v, b_v, head_dim):
    n_rows, d_model = hidden.shape
    q_cols, kv_cols = w_q.shape[1], w_k.shape[1]
    tile = 512
    n_tiles = q_cols // tile
    n_heads, n_groups = q_cols // head_dim, kv_cols // head_dim
    last = n_tiles - 1
    whole = lambda shape: pl.BlockSpec(shape, lambda i: (0,) * len(shape))
    return pl.pallas_call(
        functools.partial(qkv_kernel, n_tiles, head_dim),
        grid=(n_tiles + 1,),
        in_specs=[whole((n_rows, d_model)), whole((1, d_model)), whole((n_rows, head_dim)), whole((n_rows, head_dim)),
                  pl.BlockSpec((d_model, tile), lambda i: (0, jnp.minimum(i, last))),
                  pl.BlockSpec((1, 1, tile), lambda i: (jnp.minimum(i, last), 0, 0)),
                  ANY_SPEC, whole((1, kv_cols)), ANY_SPEC, whole((1, kv_cols))],
        out_specs=[pl.BlockSpec((n_rows * tile // head_dim, head_dim), lambda i: (jnp.minimum(i, last), 0)),
                   whole((n_groups * n_rows, head_dim)), whole((n_groups * n_rows, head_dim)),
                   whole((n_rows, kv_cols)), whole((n_rows, kv_cols))],
        out_shape=[jax.ShapeDtypeStruct((n_heads * n_rows, head_dim), F32),
                   jax.ShapeDtypeStruct((n_groups * n_rows, head_dim), F32),
                   jax.ShapeDtypeStruct((n_groups * n_rows, head_dim), F32),
                   jax.ShapeDtypeStruct((n_rows, kv_cols), BF16), jax.ShapeDtypeStruct((n_rows, kv_cols), BF16)],
        scratch_shapes=[pltpu.VMEM((n_rows, d_model), BF16), pltpu.VMEM((d_model, kv_cols), BF16),
                        pltpu.VMEM((d_model, kv_cols), BF16), pltpu.SemaphoreType.DMA((2,))],
        compiler_params=pltpu.CompilerParams(dimension_semantics=("arbitrary",), vmem_limit_bytes=48 * 2 ** 20),
        name="qkv",
    )(hidden, norm_w.astype(F32).reshape(1, d_model), cos_t, sin_t, w_q, b_q.astype(F32).reshape(n_tiles, 1, tile),
      w_k, b_k.astype(F32).reshape(1, kv_cols), w_v, b_v.astype(F32).reshape(1, kv_cols))


def attn_kernel(n_rows, n_heads, n_groups, block_rows, lens_ref, q_ref, kn_ref, vn_ref, k_ref, v_ref, o_ref):
    step = pl.program_id(0)
    shard = lax.axis_index('sp')
    per_row = k_ref.shape[0] // block_rows
    s_dev = per_row // n_groups
    head_dim = k_ref.shape[1]
    scale = head_dim ** -0.5
    unroll = 8
    per_group = n_heads // n_groups
    col = lax.broadcasted_iota(jnp.int32, (n_heads, per_row), 1)
    head = lax.broadcasted_iota(jnp.int32, (n_heads, per_row), 0)
    cache_pos = jnp.where(col % n_groups == head // per_group, col // n_groups + shard * s_dev, jnp.int32(2 ** 30))
    head_d = lax.broadcasted_iota(jnp.int32, (n_heads, head_dim), 0)
    lane_d = lax.broadcasted_iota(jnp.int32, (n_heads, head_dim), 1)
    new_bias = jnp.where(shard == 0, 0.0, NEG_BIG).astype(F32)
    new_gate = jnp.where(shard == 0, 1.0, 0.0).astype(F32)

    def one_row(half, row, ml):
        local = half * HALF + row
        b = step * block_rows + local
        q = q_ref[pl.ds(b, n_heads, stride=n_rows), :]
        k_new = kn_ref[pl.ds(b, 1), :]
        v_new = vn_ref[pl.ds(b, 1), :]
        for g in range(1, n_groups):
            k_new = jnp.where(head_d < g * per_group, k_new, kn_ref[pl.ds(g * n_rows + b, 1), :])
            v_new = jnp.where(head_d < g * per_group, v_new, vn_ref[pl.ds(g * n_rows + b, 1), :])
        cache = pl.ds(pl.multiple_of(local * per_row, per_row), per_row)
        s = lax.dot_general(q.astype(BF16), k_ref[cache, :], (((1,), (1,)), ((), ())), preferred_element_type=F32) * scale
        valid = cache_pos < lens_ref[b]
        s = jnp.where(valid, s, NEG_BIG)
        s_new = jnp.sum(q * k_new, axis=1, keepdims=True) * scale + new_bias
        m = jnp.maximum(jnp.max(s, axis=1, keepdims=True), s_new)
        p = jnp.where(valid, jnp.exp(s - m), 0.0)
        p_new = jnp.exp(s_new - m) * new_gate
        l = jnp.sum(p, axis=1, keepdims=True) + p_new
        o = jnp.dot(p.astype(BF16), v_ref[cache, :], preferred_element_type=F32) + p_new * v_new
        o_ref[half, row] = o
        ml = jnp.where(lane_d == row, m, ml)
        return jnp.where(lane_d == row + head_dim // 2, l, ml)

    def one_half(half, carry):
        def rows(i, ml):
            for j in range(unroll):
                ml = one_row(half, i * unroll + j, ml)
            return ml
        o_ref[half, HALF] = lax.fori_loop(0, HALF // unroll, rows, jnp.zeros((n_heads, head_dim), F32))
        return carry
    lax.fori_loop(0, block_rows // HALF, one_half, 0)


def local_attention(seq_lens, q, k_new, v_new, k_loc, v_loc, n_heads, n_groups):
    n_rows = seq_lens.shape[0]
    head_dim = q.shape[1]
    block_rows = 32
    per_row = k_loc.shape[0] // n_rows
    whole = lambda shape: pl.BlockSpec(shape, lambda i, lens: (0,) * len(shape))
    cache_spec = pl.BlockSpec((block_rows * per_row, head_dim), lambda i, lens: (i, 0))
    n_halves = n_rows // HALF
    return pl.pallas_call(
        functools.partial(attn_kernel, n_rows, n_heads, n_groups, block_rows),
        grid_spec=pltpu.PrefetchScalarGridSpec(
            num_scalar_prefetch=1, grid=(n_rows // block_rows,),
            in_specs=[whole(q.shape), whole(k_new.shape), whole(v_new.shape), cache_spec, cache_spec],
            out_specs=pl.BlockSpec((block_rows // HALF, ML_ROWS, n_heads, head_dim), lambda i, lens: (i, 0, 0, 0))),
        out_shape=jax.ShapeDtypeStruct((n_halves, ML_ROWS, n_heads, head_dim), F32),
        compiler_params=pltpu.CompilerParams(dimension_semantics=("arbitrary",), vmem_limit_bytes=40 * 2 ** 20),
        name="attn",
    )(seq_lens, q, k_new, v_new, k_loc, v_loc)


def combine(dst, terms):
    planes = [t[HALF] for t in terms]
    shape = planes[0].shape
    lane = lax.broadcasted_iota(jnp.int32, shape, 1)
    top = functools.reduce(jnp.maximum, planes)
    factors = [jnp.exp(p - top) for p in planes]
    sums = sum(p * pltpu.roll(f, shape[1] // 2, 1) for p, f in zip(planes, factors))
    for r in range(HALF):
        dst[r] = sum(t[r] * f[:, r:r + 1] for t, f in zip(terms, factors))
    dst[HALF] = jnp.where(lane < shape[1] // 2, top, sums)


def finish_kernel(n_sp, n_tp, o_ref, hid_ref, wo_ref, out_ref, recv1, comb, d2, from_l, from_r, attn, lhs, w_buf, hid_buf,
                  part, yd2, y_l, y_r, y_buf, send1, recv1_sem, send2, recv2, send3, recv3, send4, recv4, send_d, recv_d,
                  load_sem):
    dp, t, s = lax.axis_index('dp'), lax.axis_index('tp'), lax.axis_index('sp')
    nx = n_sp // 2
    x, c = s // 2, s % 2
    peer = 1 - c
    n_heads, head_dim = o_ref.shape[2], o_ref.shape[3]
    blk_rows = 4 * HALF
    tile = part.shape[2]

    def at(ty, sx, core):
        return (dp, lax.rem(ty + n_tp, n_tp), lax.rem(sx + nx, nx) * 2 + core)

    partner = at(t, x, peer)
    right, left = at(t, x + 1, c), at(t, x - 1, c)
    up, down = at(t + 1, x, c), at(t - 1, x, c)

    def remote(src, dst, ssem, rsem, dev):
        copy = pltpu.make_async_remote_copy(src_ref=src, dst_ref=dst, send_sem=ssem, recv_sem=rsem, device_id=dev,
                                            device_id_type=MESH)
        copy.start()
        return copy

    col0 = c * (n_tp * tile)
    loads = []
    for dt in (2, 1, 3, 0):
        cols = pl.ds(pl.multiple_of(col0 + lax.rem(t + dt, n_tp) * tile, tile), tile)
        loads.append(pltpu.make_async_copy(wo_ref.at[:, cols], w_buf.at[dt], load_sem.at[dt]))
    my_cols = pl.ds(pl.multiple_of(col0 + t * tile, tile), tile)
    my_rows = pl.ds(pl.multiple_of(x * blk_rows, blk_rows), blk_rows)
    loads.append(pltpu.make_async_copy(hid_ref.at[my_rows, my_cols], hid_buf, load_sem.at[4]))
    for load in loads:
        load.start()

    barrier = pltpu.get_barrier_semaphore()
    for dev in (partner, right, left, up, down):
        pl.semaphore_signal(barrier, inc=1, device_id=dev, device_id_type=MESH)
    pl.semaphore_wait(barrier, 5)

    def block_of(dx, core):
        return (lax.rem(x + dx, nx) * 2 + core) * 2
    order = (2, 1, 3, 0)
    first = {dx: remote(o_ref.at[pl.ds(block_of(dx, peer), 2)], recv1.at[dx], send1.at[dx], recv1_sem.at[dx], partner)
             for dx in order}

    def join(dx):
        first[dx].wait_recv()
        for h in range(2):
            combine(comb.at[dx, h], [o_ref.at[block_of(dx, c) + h], recv1.at[dx, h]])

    sends = []
    join(2)
    far_r = remote(comb.at[2, 0], d2.at[0], send2.at[0], recv2.at[0], right)
    far_l = remote(comb.at[2, 1], d2.at[1], send2.at[1], recv2.at[1], left)
    join(1)
    near_r1 = remote(comb.at[1, 1], from_l.at[1], send2.at[2], recv2.at[2], right)
    join(3)
    near_l0 = remote(comb.at[3, 0], from_r.at[0], send2.at[3], recv2.at[3], left)
    join(0)
    far_r.wait_recv()
    combine(comb.at[4, 0], [comb.at[1, 0], d2.at[0]])
    near_r0 = remote(comb.at[4, 0], from_l.at[0], send2.at[4], recv2.at[4], right)
    far_l.wait_recv()
    combine(comb.at[4, 1], [comb.at[3, 1], d2.at[1]])
    near_l1 = remote(comb.at[4, 1], from_r.at[1], send2.at[5], recv2.at[5], left)
    sends += list(first.values()) + [far_r, far_l, near_r1, near_l0, near_r0, near_l1]

    for copy in (near_r1, near_l0, near_r0, near_l1):
        copy.wait_recv()
    for h in range(2):
        combine(recv1.at[0, h], [comb.at[0, h], from_l.at[h], from_r.at[h]])
        plane = recv1[0, h, HALF]
        for r in range(HALF):
            total = recv1[0, h, r]
            attn[c, h * HALF + r] = (total / plane[:, head_dim // 2 + r:head_dim // 2 + r + 1]).astype(BF16).astype(F32)
    share = remote(attn.at[c], attn.at[c], send3.at[0], recv3.at[0], partner)
    sends.append(share)
    share.wait_recv()
    flat = 2 * HALF
    for core in range(2):
        for h in range(n_heads):
            lhs[core * flat:(core + 1) * flat, h * head_dim:(h + 1) * head_dim] = attn[core, :, h, :].astype(BF16)

    half_rows = blk_rows // 2
    lo, hi = pl.ds(0, half_rows), pl.ds(half_rows, half_rows)

    def project(i, dt):
        loads[i].wait()
        part[dt] = jnp.dot(lhs[...], w_buf[dt], preferred_element_type=F32)
    project(0, 2)
    yfar_u = remote(part.at[2, lo], yd2.at[0], send3.at[1], recv3.at[1], up)
    yfar_d = remote(part.at[2, hi], yd2.at[1], send3.at[2], recv3.at[2], down)
    project(1, 1)
    ynear_u1 = remote(part.at[1, hi], y_l.at[1], send3.at[3], recv3.at[3], up)
    project(2, 3)
    ynear_d0 = remote(part.at[3, lo], y_r.at[0], send3.at[4], recv3.at[4], down)
    project(3, 0)
    yfar_u.wait_recv()
    part[4, lo] = part[1, lo] + yd2[0]
    ynear_u0 = remote(part.at[4, lo], y_l.at[0], send3.at[5], recv3.at[5], up)
    yfar_d.wait_recv()
    part[4, hi] = part[3, hi] + yd2[1]
    ynear_d1 = remote(part.at[4, hi], y_r.at[1], send3.at[6], recv3.at[6], down)
    sends += [yfar_u, yfar_d, ynear_u1, ynear_d0, ynear_u0, ynear_d1]
    loads[4].wait()
    for h, (from_d, from_u) in enumerate(((ynear_u0, ynear_d0), (ynear_u1, ynear_d1))):
        from_d.wait_recv()
        from_u.wait_recv()
        rows = pl.ds(h * half_rows, half_rows)
        total = part[0, rows] + y_l[h] + y_r[h] + hid_buf[rows, :].astype(F32)
        y_buf[c, t, x, rows] = total.astype(BF16).astype(F32)

    ici, d2d = [0], [0]
    waits_d = []

    def hop(ty, sx, start, rows, dev):
        piece = y_buf.at[c, lax.rem(ty + n_tp, n_tp), lax.rem(sx + nx, nx), pl.ds(start, rows)]
        i = ici[0]
        ici[0] += 1
        copy = remote(piece, piece, send4.at[i], recv4.at[i], dev)
        sends.append(copy)
        return copy

    def to_partner(ty, sx, start, rows):
        piece = y_buf.at[c, lax.rem(ty + n_tp, n_tp), lax.rem(sx + nx, nx), pl.ds(start, rows)]
        i = d2d[0]
        d2d[0] += 1
        copy = remote(piece, piece, send_d.at[i], recv_d.at[i], partner)
        sends.append(copy)
        waits_d.append(copy)

    quarter = half_rows // 2
    plans = (('y', 0), ('x', half_rows))

    def off(axis, d):
        return (d, 0) if axis == 'y' else (0, d)
    devs = {('y', 1): up, ('y', -1): down, ('x', 1): right, ('x', -1): left}
    other = {'y': 'x', 'x': 'y'}

    def start_piece(axis, base, start):
        ty, sx = t + base[0], x + base[1]
        return (hop(ty, sx, start, half_rows, devs[axis, 1]), hop(ty, sx, start, half_rows, devs[axis, -1]))

    def pass_on(axis, base, start, pair):
        far = []
        for way, (copy, lead) in enumerate(zip(pair, (-1, 1))):
            copy.wait_recv()
            d = off(axis, lead)
            far.append(hop(t + base[0] + d[0], x + base[1] + d[1], start + way * quarter, quarter, devs[axis, -lead]))
        return far

    firsts = {}
    for axis, start in plans:
        firsts[axis] = start_piece(axis, (0, 0), start)
    seconds = {}
    for axis, start in plans:
        seconds[axis, 0] = start_piece(other[axis], (0, 0), start)
        to_partner(t, x, start, half_rows)
    fars = {}
    for axis, start in plans:
        fars[axis] = pass_on(axis, (0, 0), start, firsts[axis])
    for axis, start in plans:
        for lead in (-1, 1):
            d = off(axis, lead)
            seconds[axis, lead] = start_piece(other[axis], d, start)
            to_partner(t + d[0], x + d[1], start, half_rows)
    for axis, start in plans:
        for copy in fars[axis]:
            copy.wait_recv()
        d = off(axis, 2)
        seconds[axis, 2] = start_piece(other[axis], d, start)
        to_partner(t + d[0], x + d[1], start, half_rows)
    last = {}
    for lead in (0, -1, 1, 2):
        for axis, start in plans:
            base = off(axis, lead)
            last[axis, lead] = pass_on(other[axis], base, start, seconds[axis, lead])
            for d in (off(other[axis], -1), off(other[axis], 1)):
                to_partner(t + base[0] + d[0], x + base[1] + d[1], start, half_rows)
    for lead in (0, -1, 1, 2):
        for axis, start in plans:
            base, d = off(axis, lead), off(other[axis], 2)
            for copy in last[axis, lead]:
                copy.wait_recv()
            to_partner(t + base[0] + d[0], x + base[1] + d[1], start, half_rows)
    for copy in waits_d:
        copy.wait_recv()

    def write(i, carry):
        core, ty, sx = i // (n_tp * nx), (i // nx) % n_tp, i % nx
        rows = pl.ds(pl.multiple_of(sx * blk_rows, blk_rows), blk_rows)
        cols = pl.ds(pl.multiple_of(core * (n_tp * tile) + ty * tile, tile), tile)
        out_ref[rows, cols] = y_buf[core, ty, sx].astype(BF16)
        return carry
    lax.fori_loop(0, 2 * n_tp * nx, write, 0)
    for copy in sends:
        copy.wait_send()


def finish(o_parts, hidden, w_o, n_sp, n_tp):
    n_rows, d_model = hidden.shape
    n_halves, _, n_heads, head_dim = o_parts.shape
    nx = n_sp // 2
    tile = d_model // (2 * n_tp)
    blk = 4 * HALF
    half_shape = (ML_ROWS, n_heads, head_dim)
    dma = pltpu.SemaphoreType.DMA
    return pl.pallas_call(
        functools.partial(finish_kernel, n_sp, n_tp),
        in_specs=[VMEM_SPEC, ANY_SPEC, ANY_SPEC],
        out_specs=VMEM_SPEC,
        out_shape=jax.ShapeDtypeStruct((n_rows, d_model), BF16),
        scratch_shapes=[
            pltpu.VMEM((nx, 2) + half_shape, F32), pltpu.VMEM((nx + 1, 2) + half_shape, F32),
            pltpu.VMEM((2,) + half_shape, F32), pltpu.VMEM((2,) + half_shape, F32), pltpu.VMEM((2,) + half_shape, F32),
            pltpu.VMEM((2, 2 * HALF, n_heads, head_dim), F32), pltpu.VMEM((blk, n_heads * head_dim), BF16),
            pltpu.VMEM((n_tp, n_heads * head_dim, tile), BF16), pltpu.VMEM((blk, tile), BF16),
            pltpu.VMEM((n_tp + 1, blk, tile), F32), pltpu.VMEM((2, blk // 2, tile), F32),
            pltpu.VMEM((2, blk // 2, tile), F32), pltpu.VMEM((2, blk // 2, tile), F32),
            pltpu.VMEM((2, n_tp, nx, blk, tile), F32),
            dma((4,)), dma((4,)), dma((6,)), dma((6,)), dma((7,)), dma((7,)), dma((40,)), dma((40,)), dma((32,)), dma((32,)),
            dma((5,))],
        compiler_params=pltpu.CompilerParams(collective_id=0, has_side_effects=True, vmem_limit_bytes=60 * 2 ** 20),
        name="finish",
    )(o_parts, hidden, w_o)


def solution(mesh):
    n_sp, n_tp = mesh.shape['sp'], mesh.shape['tp']

    def device_step(hidden, norm_w, w_q, b_q, w_k, b_k, w_v, b_v, w_o, k_cache, v_cache, positions, seq_lens):
        n_rows = hidden.shape[0]
        groups_dev, head_dim = k_cache.shape[2], k_cache.shape[3]
        heads_dev = w_q.shape[1] // head_dim
        rot_dim = head_dim // 2
        lane = jnp.arange(head_dim, dtype=jnp.int32)
        inv_freq = ROPE_BASE ** (-2.0 * (lane // 2).astype(F32) / rot_dim)
        angles = positions.astype(F32)[:, None] * inv_freq
        cos_t = jnp.cos(angles)
        sin_t = jnp.where(lane % 2 == 0, -jnp.sin(angles), jnp.sin(angles))
        q, k_rot, v_row, k_out, v_out = qkv_project(hidden, norm_w, cos_t, sin_t, w_q, b_q, w_k, b_k, w_v, b_v, head_dim)
        o_parts = local_attention(seq_lens, q, k_rot, v_row, k_cache.reshape(-1, head_dim), v_cache.reshape(-1, head_dim),
                                  heads_dev, groups_dev)
        y_out = finish(o_parts, hidden, w_o, n_sp, n_tp)
        return y_out, k_out.reshape(n_rows, groups_dev, head_dim), v_out.reshape(n_rows, groups_dev, head_dim)

    col_spec = P(None, 'tp')
    vec_spec = P('tp')
    cache_spec = P('dp', 'sp', 'tp', None)
    group_spec = P('dp', 'tp', None)
    in_specs = (P('dp', None), P(None), col_spec, vec_spec, col_spec, vec_spec, col_spec, vec_spec,
                P('tp', None), cache_spec, cache_spec, P('dp'), P('dp'))
    out_specs = (P('dp', None), group_spec, group_spec)
    return jax.shard_map(device_step, mesh=mesh, in_specs=in_specs, out_specs=out_specs, check_vma=False)
```

time: 293 us -> 161 us (0.55)
  Pallas kernels: 0 us -> 144 us
  waiting for transfers between devices: 128 us -> 0 us
  blocking collectives: 55.8 us -> 0 us
  matrix products: 54.7 us -> 0 us
  other arithmetic: 24.2 us -> 3.95 us
  between operations: 14.4 us -> 0.7 us
  local copies, waits for them, and re-layouts: 15.1 us -> 11.3 us
    pallas_call x0 -> x3, Pallas kernels: none -> 144 us  [the longest x1 67.7 us: local_attention(): pl.pallas_call(functools.partial(attn_kernel, n_rows, n_heads, n_groups,...]
    psum x2 -> x0, waiting for transfers between devices: 128 us -> none  [the longest x1 87.5 us: device_step(): lax.psum(jnp.dot(attn_rows, w_o, preferred_element_type=jnp.float32), 'tp')]
    dot_general x7 -> x0, matrix products: 54.7 us -> none  [the longest x3 15.9 us: project(): jnp.dot(normed, weight, preferred_element_type=jnp.float32)]
    psum x1 -> x0, blocking collectives: 29.1 us -> none  [device_step(): l_all, o_all = lax.psum((l_loc * factor, o_loc * factor[..., None]), 'sp')]
    pmax x1 -> x0, blocking collectives: 26.7 us -> none  [device_step(): m_all = lax.pmax(m_loc, 'sp')]
    convert_element_type x7 -> x1, other arithmetic: 11.1 us -> 0.68 us  [device_step(): angles = positions.astype(F32)[:, None] * inv_freq]
    reduce_sum x2 -> x0, other arithmetic: 9.65 us -> none  [the longest x1 7.42 us: local_partials(): l_loc = jnp.sum(p_cache, axis=-1) + p_new]
    unnamed x22 -> x11, local copies, waits for them, and re-layouts: 6.74 us -> 9.9 us
  transfers between devices with their start and end apart: 2 -> 0, of which waited for: 2 -> 0; matrix products, arithmetic and copies ran while one was open for 1% -> 0% of each run, Pallas kernels for 0% -> 0%
where the time goes in v1:
time: 161 us; the launch traced here: 160 us
  Pallas kernels  144 us (89%)
  local copies, waits for them, and re-layouts  11.3 us (7%)
  other arithmetic  3.95 us (2%)
    pallas_call x1, Pallas kernels, local_attention(): pl.pallas_call(functools.partial(attn_kernel, n_rows, n_heads, n_groups,...  67.7 us
    pallas_call x1, Pallas kernels, finish(): pl.pallas_call(functools.partial(finish_kernel, n_sp, n_tp), in_specs=[VM...  59 us
    pallas_call x1, Pallas kernels, qkv_project(): pl.pallas_call(functools.partial(qkv_kernel, n_tiles, head_dim), grid=(n_...  17.8 us
    unnamed x11, local copies, waits for them, and re-layouts  9.9 us

profile of v1, /device:TPU:97, one launch (start us, length us, event | category | flops | bytes accessed | tf_op | source)
XLA Modules:
  0.0 160.4 jit_solution(17721274248565993169)
XLA Ops:
  0.7 0.7 reshape.71
  1.3 0.7 reshape.73
  2.0 0.7 convert_element_type.14
  2.7 0.7 reshape.69
  3.3 0.7 reshape.67
  4.0 0.5 negate_select_fusion
  4.6 0.0 copy-start.1
  4.6 1.6 copy-done.1
  6.2 0.0 copy-start.3
  6.2 1.6 copy-done.3
  7.8 0.0 copy-start.4
  7.8 17.8 %qkv.1 = (f32[6144,128]{1,0:T(8,128)}, f32[512,128]{1,0:T(8,128)S(1)}, f32[512,128]{1,0:T(8,128)S(1)}, bf16[256,256]{1,0:T(8,128)(2,1)S(1)}, bf16[256,256]{1,0:T(8,128)(2,1)S(1)}) custom-call(bf16[256,4096]{1,0:T(8,128)(2,1)S(1)} %copy-done.1, f32[1,4096]{1,0:T(1,128)S(1)} %bitcast.6, f32[256,128]{1,0:T(8,128)S(1)} %get-tuple-element.14.cos_ref, ...), custom_call_target="tpu_custom_call" | custom-call | tf_op jit(solution)/shard_map/qkv/pallas_call | solution.py:83
  25.6 0.0 copy-done.4
  25.6 0.0 copy-start.2
  25.6 1.9 %copy-done.2 = f32[6144,128]{1,0:T(8,128)S(1)} copy-done((f32[6144,128]{1,0:T(8,128)S(1)}, f32[6144,128]{1,0:T(8,128)}, u32[]{:S(2)}) %copy-start.2) | copy-done | bytes 3145752
  27.5 67.7 %attn.1.o_ref = f32[16,17,24,128]{3,2,1,0:T(8,128)S(1)} custom-call(s32[256]{0:T(256)S(1)} %copy-done.4, f32[6144,128]{1,0:T(8,128)S(1)} %copy-done.2, f32[512,128]{1,0:T(8,128)S(1)} %get-tuple-element.9.kn_ref, f32[512,128]{1,0:T(8,128)S(1)} %get-tuple-element.10.vn_ref, bf16[65536,128]{1,0:T(8,128)(2,1)} %bitcast.10, bf16[65536,128]{1,0:T(8,128)(2,1)} %bitcast.11), custom_call_target="tpu_custom_call" | custom-call | tf_op jit(solution)/shard_map/attn/pallas_call | solution.py:163
  95.2 0.0 copy-start
  95.2 1.7 %copy-done = f32[16,17,24,128]{3,2,1,0:T(8,128)} copy-done((f32[16,17,24,128]{3,2,1,0:T(8,128)}, f32[16,17,24,128]{3,2,1,0:T(8,128)S(1)}, u32[]{:S(2)}) %copy-start) | copy-done | bytes 3342360
  96.9 59.0 %finish.1 = bf16[256,4096]{1,0:T(8,128)(2,1)} custom-call(f32[16,17,24,128]{3,2,1,0:T(8,128)} %copy-done, bf16[256,4096]{1,0:T(8,128)(2,1)} %hid_ref.3, bf16[3072,4096]{1,0:T(8,128)(2,1)} %wo_ref.1), custom_call_target="tpu_custom_call" | custom-call | tf_op jit(solution)/shard_map/finish/pallas_call | solution.py:395
  155.9 0.7 reshape.65
  156.6 0.7 reshape.66
  157.3 3.1 %copy.17 = bf16[256,4096]{1,0:T(8,128)(2,1)} copy(bf16[256,4096]{1,0:T(8,128)(2,1)} %finish.1) | data formatting | bytes 4194304
  (2 shorter events, 0.0 us)
Async XLA Ops:
  4.6 1.6 copy-start.1
  6.2 1.6 copy-start.3
  7.8 17.8 %copy-start.4 = (s32[256]{0:T(256)S(1)}, s32[256]{0:T(256)}, u32[]{:S(2)}) copy-start(s32[256]{0:T(256)} %lens_ref.1) | copy-start | bytes 3076
  25.6 1.9 %copy-start.2 = (f32[6144,128]{1,0:T(8,128)S(1)}, f32[6144,128]{1,0:T(8,128)}, u32[]{:S(2)}) copy-start(f32[6144,128]{1,0:T(8,128)} %get-tuple-element.8.q_ref) | copy-start | bytes 9437188
  95.2 1.7 %copy-start = (f32[16,17,24,128]{3,2,1,0:T(8,128)}, f32[16,17,24,128]{3,2,1,0:T(8,128)S(1)}, u32[]{:S(2)}) copy-start(f32[16,17,24,128]{3,2,1,0:T(8,128)S(1)} %attn.1.o_ref) | copy-start | bytes 10027012

commit v2 on v1

v2 whole, which is shorter than its diff:
```python
import functools

import jax
import jax.numpy as jnp
from jax import lax
from jax.experimental import pallas as pl
from jax.experimental.pallas import tpu as pltpu
from jax.sharding import PartitionSpec as P

RMS_EPS = 1.5625e-7
ROPE_BASE = 10000.0
NEG_BIG = -1e30
F32 = jnp.float32
BF16 = jnp.bfloat16
MESH = pl.DeviceIdType.MESH
HALF = 16
ML_ROWS = HALF + 1
VMEM_SPEC = pl.BlockSpec(memory_space=pltpu.VMEM)
ANY_SPEC = pl.BlockSpec(memory_space=pl.ANY)


def rope(heads, cos_t, sin_t):
    lane = lax.broadcasted_iota(jnp.int32, heads.shape, 1)
    width = heads.shape[1]
    swapped = jnp.where(lane % 2 == 0, pltpu.roll(heads, width - 1, 1), pltpu.roll(heads, 1, 1))
    rotated = (heads * cos_t + swapped * sin_t).astype(BF16).astype(F32)
    return jnp.where(lane < width // 2, rotated, heads)


def combine(dst, terms):
    planes = [t[HALF] for t in terms]
    shape = planes[0].shape
    lane = lax.broadcasted_iota(jnp.int32, shape, 1)
    top = functools.reduce(jnp.maximum, planes)
    factors = [jnp.exp(p - top) for p in planes]
    sums = sum(p * pltpu.roll(f, shape[1] // 2, 1) for p, f in zip(planes, factors))
    for r in range(HALF):
        dst[r] = sum(t[r] * f[:, r:r + 1] for t, f in zip(terms, factors))
    dst[HALF] = jnp.where(lane < shape[1] // 2, top, sums)


GROUP = 8
SLOTS = 6


def step_kernel(n_sp, n_tp, n_groups, lens_ref, hid_ref, vec_ref, cos_ref, sin_ref, wq_ref, wk_ref, wv_ref, wo_ref, k_ref,
                v_ref, out_ref, kb_ref, vb_ref, hid, w_buf, wk_buf, wv_buf, q_scr, kn, vn, k_buf, v_buf, s_buf, o_scr,
                recv1, comb, d2, from_l, from_r, attn, lhs, hid_buf, part, yd2, y_l, y_r, y_buf, load_sem, kv_sem,
                sendq, recvq, send1, recv1_sem, send2, recv2, send3, recv3, send4, recv4, send_d, recv_d):
    dp, t, s = lax.axis_index('dp'), lax.axis_index('tp'), lax.axis_index('sp')
    nx = n_sp // 2
    x, c = s // 2, s % 2
    peer = 1 - c
    n_rows, d_model = hid.shape
    head_dim = q_scr.shape[1]
    n_heads = q_scr.shape[0] // n_rows
    per_group = n_heads // n_groups
    per_row = k_buf.shape[1] // HALF
    s_dev = per_row // n_groups
    tile = w_buf.shape[1]
    q_tiles = n_heads * head_dim // (2 * tile)
    heads_tile = tile // head_dim
    blk_rows = 4 * HALF
    scale = head_dim ** -0.5

    def at(ty, sx, core):
        return (dp, lax.rem(ty + n_tp, n_tp), lax.rem(sx + nx, nx) * 2 + core)

    partner = at(t, x, peer)
    right, left = at(t, x + 1, c), at(t, x - 1, c)
    up, down = at(t + 1, x, c), at(t - 1, x, c)

    def remote_copy(src, dst, ssem, rsem, dev):
        return pltpu.make_async_remote_copy(src_ref=src, dst_ref=dst, send_sem=ssem, recv_sem=rsem, device_id=dev,
                                            device_id_type=MESH)

    def remote(*args):
        copy = remote_copy(*args)
        copy.start()
        return copy

    load_hid = pltpu.make_async_copy(hid_ref, hid, load_sem.at[0])
    load_q = [pltpu.make_async_copy(wq_ref.at[:, pl.ds(pl.multiple_of((c * q_tiles + i) * tile, tile), tile)],
                                    w_buf.at[pl.ds(i * d_model, d_model)], load_sem.at[1 + i]) for i in range(q_tiles)]
    my_group = pl.ds(pl.multiple_of(c * head_dim, head_dim), head_dim)
    load_k = pltpu.make_async_copy(wk_ref.at[:, my_group], wk_buf, load_sem.at[1 + q_tiles])
    load_v = pltpu.make_async_copy(wv_ref.at[:, my_group], wv_buf, load_sem.at[2 + q_tiles])
    load_hid.start()
    for load in load_q:
        load.start()
    load_k.start()
    load_v.start()
    my_cols = pl.ds(pl.multiple_of((c * n_tp + t) * tile, tile), tile)
    my_rows = pl.ds(pl.multiple_of(x * blk_rows, blk_rows), blk_rows)
    load_res = pltpu.make_async_copy(hid_ref.at[my_rows, my_cols], hid_buf, load_sem.at[3 + q_tiles])
    load_res.start()

    barrier = pltpu.get_barrier_semaphore()
    for dev in (partner, right, left, up, down):
        pl.semaphore_signal(barrier, inc=1, device_id=dev, device_id_type=MESH)

    def half_block(i, j):
        k = i // 2
        side = jnp.where(j == 0, 1, 3)
        dx = jnp.where(k == 0, 2, jnp.where(k == 3, 0, side))
        h = jnp.where(k == 1, 1 - j, j)
        core = jnp.where(i % 2 == 0, peer, c)
        return (lax.rem(x + dx, nx) * 2 + core) * 2 + h

    def cache_copies(i, j):
        slot = lax.rem(i * 2 + j, SLOTS)
        rows = pl.ds(pl.multiple_of(half_block(i, j) * (HALF * per_row), HALF * per_row), HALF * per_row)
        return (pltpu.make_async_copy(k_ref.at[rows], k_buf.at[slot], kv_sem.at[slot * 2]),
                pltpu.make_async_copy(v_ref.at[rows], v_buf.at[slot], kv_sem.at[slot * 2 + 1]))

    def start_cache(i):
        for j in range(2):
            for copy in cache_copies(i, j):
                copy.start()

    def wait_cache(i):
        for j in range(2):
            for copy in cache_copies(i, j):
                copy.wait()

    load_hid.wait()

    def norm_rows(i, carry):
        rows = pl.ds(pl.multiple_of(i * 16, 16), 16)
        xr = hid[rows, :].astype(F32)
        mean_sq = jnp.mean(xr * xr, axis=1, keepdims=True)
        hid[rows, :] = (xr * lax.rsqrt(mean_sq + RMS_EPS) * vec_ref[:, :d_model]).astype(BF16)
        return carry
    lax.fori_loop(0, n_rows // 16, norm_rows, 0)
    for i in range(SLOTS // 2):
        start_cache(i)

    pl.semaphore_wait(barrier, 5)
    shared = []
    for i in range(q_tiles):
        load_q[i].wait()
        first = (c * q_tiles + i) * heads_tile
        bias = vec_ref[:, pl.ds(pl.multiple_of(d_model + first * head_dim, head_dim), tile)]
        acc = jnp.dot(hid[...], w_buf[i * d_model:(i + 1) * d_model, :], preferred_element_type=F32) + bias
        acc = acc.astype(BF16).astype(F32)
        for h in range(heads_tile):
            rows = pl.ds(pl.multiple_of((first + h) * n_rows, n_rows), n_rows)
            q_scr[rows, :] = rope(acc[:, h * head_dim:(h + 1) * head_dim], cos_ref[...], sin_ref[...])
        piece = q_scr.at[pl.ds(pl.multiple_of(first * n_rows, n_rows), heads_tile * n_rows)]
        shared.append(remote(piece, piece, sendq.at[i], recvq.at[i], partner))
    load_k.wait()
    load_v.wait()
    rows = pl.ds(pl.multiple_of(c * n_rows, n_rows), n_rows)
    bias_at = d_model + n_heads * head_dim + c * head_dim
    b_k = vec_ref[:, pl.ds(pl.multiple_of(bias_at, head_dim), head_dim)]
    b_v = vec_ref[:, pl.ds(pl.multiple_of(bias_at + n_groups * head_dim, head_dim), head_dim)]
    k_row = (jnp.dot(hid[...], wk_buf[...], preferred_element_type=F32) + b_k).astype(BF16).astype(F32)
    kn[rows, :] = rope(k_row, cos_ref[...], sin_ref[...])
    shared.append(remote(kn.at[rows], kn.at[rows], sendq.at[q_tiles], recvq.at[q_tiles], partner))
    vn[rows, :] = (jnp.dot(hid[...], wv_buf[...], preferred_element_type=F32) + b_v).astype(BF16).astype(F32)
    shared.append(remote(vn.at[rows], vn.at[rows], sendq.at[q_tiles + 1], recvq.at[q_tiles + 1], partner))
    for copy in shared:
        copy.wait_recv()

    col = lax.broadcasted_iota(jnp.int32, (n_heads, per_row), 1)
    head = lax.broadcasted_iota(jnp.int32, (n_heads, per_row), 0)
    cache_pos = jnp.where(col % n_groups == head // per_group, col // n_groups + s * s_dev, jnp.int32(2 ** 30))
    head_d = lax.broadcasted_iota(jnp.int32, (n_heads, head_dim), 0)
    lane_d = lax.broadcasted_iota(jnp.int32, (n_heads, head_dim), 1)
    new_bias = jnp.where(s == 0, 0.0, NEG_BIG).astype(F32)
    new_gate = jnp.where(s == 0, 1.0, 0.0).astype(F32)

    def scores(i, g):
        j = g * GROUP // HALF
        slot = lax.rem(i * 2 + j, SLOTS)
        b0 = half_block(i, j) * HALF
        for r in range(GROUP):
            row = g * GROUP % HALF + r
            q = q_scr[pl.ds(b0 + row, n_heads, stride=n_rows), :]
            k = k_buf[slot, row * per_row:(row + 1) * per_row, :]
            s_buf[g % 2, r] = lax.dot_general(q.astype(BF16), k, (((1,), (1,)), ((), ())), preferred_element_type=F32)

    def outputs(i, g, ml):
        j = g * GROUP // HALF
        slot = lax.rem(i * 2 + j, SLOTS)
        hb = half_block(i, j)
        probs = []
        for r in range(GROUP):
            row = g * GROUP % HALF + r
            b = hb * HALF + row
            q = q_scr[pl.ds(b, n_heads, stride=n_rows), :]
            k_new, v_new = kn[pl.ds(b, 1), :], vn[pl.ds(b, 1), :]
            for gr in range(1, n_groups):
                k_new = jnp.where(head_d < gr * per_group, k_new, kn[pl.ds(gr * n_rows + b, 1), :])
                v_new = jnp.where(head_d < gr * per_group, v_new, vn[pl.ds(gr * n_rows + b, 1), :])
            valid = cache_pos < lens_ref[b]
            sc = jnp.where(valid, s_buf[g % 2, r] * scale, NEG_BIG)
            s_new = jnp.sum(q * k_new, axis=1, keepdims=True) * scale + new_bias
            m = jnp.maximum(jnp.max(sc, axis=1, keepdims=True), s_new)
            p = jnp.where(valid, jnp.exp(sc - m), 0.0)
            p_new = jnp.exp(s_new - m) * new_gate
            l = jnp.sum(p, axis=1, keepdims=True) + p_new
            ml = jnp.where(lane_d == row, m, ml)
            ml = jnp.where(lane_d == row + head_dim // 2, l, ml)
            probs.append((row, p.astype(BF16), p_new * v_new))
        for row, p, extra in probs:
            v = v_buf[slot, row * per_row:(row + 1) * per_row, :]
            o_scr[hb, row] = jnp.dot(p, v, preferred_element_type=F32) + extra
        return ml

    def load_o(n):
        dt = jnp.where(n == 0, 2, jnp.where(n == 3, 0, jnp.where(n == 1, 1, 3)))
        depth = n_heads * head_dim
        cols = pl.ds(pl.multiple_of((c * n_tp + lax.rem(t + dt, n_tp)) * tile, tile), tile)
        return pltpu.make_async_copy(wo_ref.at[:, cols], w_buf.at[pl.ds(pl.multiple_of(n * depth, depth), depth)],
                                     load_sem.at[n])

    def to_core(k, j):
        return remote_copy(o_scr.at[half_block(2 * k, j)], recv1.at[k, j], send1.at[2 * k + j], recv1_sem.at[2 * k + j],
                           partner)

    far_r = remote_copy(comb.at[0, 0], d2.at[0], send2.at[0], recv2.at[0], right)
    far_l = remote_copy(comb.at[0, 1], d2.at[1], send2.at[1], recv2.at[1], left)
    near_r1 = remote_copy(comb.at[1, 0], from_l.at[1], send2.at[2], recv2.at[2], right)
    near_l0 = remote_copy(comb.at[1, 1], from_r.at[0], send2.at[3], recv2.at[3], left)
    near_r0 = remote_copy(comb.at[2, 0], from_l.at[0], send2.at[4], recv2.at[4], right)
    near_l1 = remote_copy(comb.at[2, 1], from_r.at[1], send2.at[5], recv2.at[5], left)
    n_units = n_rows // (2 * HALF)
    n_groups_unit = 2 * HALF // GROUP

    wait_cache(0)
    scores(0, 0)

    def unit(i, carry):
        nxt = jnp.minimum(i + 1, n_units - 1)

        @pl.when(i < n_units - 1)
        def _():
            wait_cache(i + 1)

        @pl.when(i < n_tp)
        def _():
            load_o(i).start()
        ml = jnp.zeros((n_heads, head_dim), F32)
        for g in range(n_groups_unit):
            if g < n_groups_unit - 1:
                scores(i, g + 1)
            else:
                scores(nxt, 0)
            ml = outputs(i, g, ml)
            if (g + 1) * GROUP % HALF == 0:
                o_scr[half_block(i, g * GROUP // HALF), HALF] = ml
                ml = jnp.zeros((n_heads, head_dim), F32)

        @pl.when(i + SLOTS // 2 < n_units)
        def _():
            start_cache(i + SLOTS // 2)

        k = i // 2

        @pl.when(i % 2 == 0)
        def _():
            for j in range(2):
                to_core(k, j).start()

        @pl.when(i % 2 == 1)
        def _():
            for j in range(2):
                to_core(k, j).wait_recv()

            @pl.when(k < 2)
            def _():
                for j in range(2):
                    combine(comb.at[k, j], [o_scr.at[half_block(i, j)], recv1.at[k, j]])

            @pl.when(k == 0)
            def _():
                far_r.start()
                far_l.start()

            @pl.when(k == 1)
            def _():
                near_r1.start()
                near_l0.start()

            @pl.when(k == 2)
            def _():
                far_r.wait_recv()
                combine(comb.at[2, 0], [o_scr.at[half_block(i, 0)], recv1.at[2, 0], d2.at[0]])
                near_r0.start()
                far_l.wait_recv()
                combine(comb.at[2, 1], [o_scr.at[half_block(i, 1)], recv1.at[2, 1], d2.at[1]])
                near_l1.start()
        return carry
    lax.fori_loop(0, n_units, unit, 0)

    for g in range(n_groups):
        cols = slice(g * head_dim, (g + 1) * head_dim)
        kb_ref[:, cols] = kn[g * n_rows:(g + 1) * n_rows, :].astype(BF16)
        vb_ref[:, cols] = vn[g * n_rows:(g + 1) * n_rows, :].astype(BF16)

    sends = shared + [to_core(k, j) for k in range(4) for j in range(2)]
    sends += [far_r, far_l, near_r1, near_l0, near_r0, near_l1]
    for h, pair in enumerate(((near_l0, near_r0), (near_r1, near_l1))):
        for copy in pair:
            copy.wait_recv()
        own = half_block(n_units - 1, h)
        combine(comb.at[3, h], [o_scr.at[own], recv1.at[3, h], from_l.at[h], from_r.at[h]])
        plane = comb[3, h, HALF]
        for r in range(HALF):
            total = comb[3, h, r]
            attn[c, h * HALF + r] = (total / plane[:, head_dim // 2 + r:head_dim // 2 + r + 1]).astype(BF16).astype(F32)
    share = remote(attn.at[c], attn.at[c], send3.at[0], recv3.at[0], partner)
    sends.append(share)
    share.wait_recv()
    flat = 2 * HALF
    for core in range(2):
        for h in range(n_heads):
            lhs[core * flat:(core + 1) * flat, h * head_dim:(h + 1) * head_dim] = attn[core, :, h, :].astype(BF16)

    half_rows = blk_rows // 2
    lo, hi = pl.ds(0, half_rows), pl.ds(half_rows, half_rows)

    def project(i, dt):
        load_o(i).wait()
        depth = n_heads * head_dim
        part[dt] = jnp.dot(lhs[...], w_buf[i * depth:(i + 1) * depth, :], preferred_element_type=F32)
    project(0, 2)
    yfar_u = remote(part.at[2, lo], yd2.at[0], send3.at[1], recv3.at[1], up)
    yfar_d = remote(part.at[2, hi], yd2.at[1], send3.at[2], recv3.at[2], down)
    project(1, 1)
    ynear_u1 = remote(part.at[1, hi], y_l.at[1], send3.at[3], recv3.at[3], up)
    project(2, 3)
    ynear_d0 = remote(part.at[3, lo], y_r.at[0], send3.at[4], recv3.at[4], down)
    project(3, 0)
    yfar_u.wait_recv()
    part[4, lo] = part[1, lo] + yd2[0]
    ynear_u0 = remote(part.at[4, lo], y_l.at[0], send3.at[5], recv3.at[5], up)
    yfar_d.wait_recv()
    part[4, hi] = part[3, hi] + yd2[1]
    ynear_d1 = remote(part.at[4, hi], y_r.at[1], send3.at[6], recv3.at[6], down)
    sends += [yfar_u, yfar_d, ynear_u1, ynear_d0, ynear_u0, ynear_d1]
    load_res.wait()
    for h, (from_d, from_u) in enumerate(((ynear_u0, ynear_d0), (ynear_u1, ynear_d1))):
        from_d.wait_recv()
        from_u.wait_recv()
        rows = pl.ds(h * half_rows, half_rows)
        total = part[0, rows] + y_l[h] + y_r[h] + hid_buf[rows, :].astype(F32)
        y_buf[c, t, x, rows] = total.astype(BF16).astype(F32)

    ici, d2d = [0], [0]
    waits_d = []

    def hop(ty, sx, start, rows, dev):
        piece = y_buf.at[c, lax.rem(ty + n_tp, n_tp), lax.rem(sx + nx, nx), pl.ds(start, rows)]
        i = ici[0]
        ici[0] += 1
        copy = remote(piece, piece, send4.at[i], recv4.at[i], dev)
        sends.append(copy)
        return copy

    def to_partner(ty, sx, start, rows):
        piece = y_buf.at[c, lax.rem(ty + n_tp, n_tp), lax.rem(sx + nx, nx), pl.ds(start, rows)]
        i = d2d[0]
        d2d[0] += 1
        copy = remote(piece, piece, send_d.at[i], recv_d.at[i], partner)
        sends.append(copy)
        waits_d.append(copy)

    quarter = half_rows // 2
    plans = (('y', 0), ('x', half_rows))

    def off(axis, d):
        return (d, 0) if axis == 'y' else (0, d)
    devs = {('y', 1): up, ('y', -1): down, ('x', 1): right, ('x', -1): left}
    other = {'y': 'x', 'x': 'y'}

    def start_piece(axis, base, start):
        ty, sx = t + base[0], x + base[1]
        return (hop(ty, sx, start, half_rows, devs[axis, 1]), hop(ty, sx, start, half_rows, devs[axis, -1]))

    def pass_on(axis, base, start, pair):
        far = []
        for way, (copy, lead) in enumerate(zip(pair, (-1, 1))):
            copy.wait_recv()
            d = off(axis, lead)
            far.append(hop(t + base[0] + d[0], x + base[1] + d[1], start + way * quarter, quarter, devs[axis, -lead]))
        return far

    firsts = {}
    for axis, start in plans:
        firsts[axis] = start_piece(axis, (0, 0), start)
    seconds = {}
    for axis, start in plans:
        seconds[axis, 0] = start_piece(other[axis], (0, 0), start)
        to_partner(t, x, start, half_rows)
    fars = {}
    for axis, start in plans:
        fars[axis] = pass_on(axis, (0, 0), start, firsts[axis])
    for axis, start in plans:
        for lead in (-1, 1):
            d = off(axis, lead)
            seconds[axis, lead] = start_piece(other[axis], d, start)
            to_partner(t + d[0], x + d[1], start, half_rows)
    for axis, start in plans:
        for copy in fars[axis]:
            copy.wait_recv()
        d = off(axis, 2)
        seconds[axis, 2] = start_piece(other[axis], d, start)
        to_partner(t + d[0], x + d[1], start, half_rows)
    last = {}
    for lead in (0, -1, 1, 2):
        for axis, start in plans:
            base = off(axis, lead)
            last[axis, lead] = pass_on(other[axis], base, start, seconds[axis, lead])
            for d in (off(other[axis], -1), off(other[axis], 1)):
                to_partner(t + base[0] + d[0], x + base[1] + d[1], start, half_rows)
    for lead in (0, -1, 1, 2):
        for axis, start in plans:
            base, d = off(axis, lead), off(other[axis], 2)
            for copy in last[axis, lead]:
                copy.wait_recv()
            to_partner(t + base[0] + d[0], x + base[1] + d[1], start, half_rows)
    for copy in waits_d:
        copy.wait_recv()

    def write(i, carry):
        core, ty, sx = i // (n_tp * nx), (i // nx) % n_tp, i % nx
        rows = pl.ds(pl.multiple_of(sx * blk_rows, blk_rows), blk_rows)
        cols = pl.ds(pl.multiple_of(core * (n_tp * tile) + ty * tile, tile), tile)
        out_ref[rows, cols] = y_buf[core, ty, sx].astype(BF16)
        return carry
    lax.fori_loop(0, 2 * n_tp * nx, write, 0)
    for copy in sends:
        copy.wait_send()


def attention_step(seq_lens, hidden, vec, cos_t, sin_t, w_q, w_k, w_v, w_o, k_loc, v_loc, n_sp, n_tp, head_dim):
    n_rows, d_model = hidden.shape
    n_heads, n_groups = w_q.shape[1] // head_dim, w_k.shape[1] // head_dim
    nx = n_sp // 2
    tile = d_model // (2 * n_tp)
    blk = 4 * HALF
    per_row = k_loc.shape[0] // n_rows
    half_shape = (ML_ROWS, n_heads, head_dim)
    q_tiles = n_heads * head_dim // (2 * tile)
    dma = pltpu.SemaphoreType.DMA
    kv_out = jax.ShapeDtypeStruct((n_rows, n_groups * head_dim), BF16)
    return pl.pallas_call(
        functools.partial(step_kernel, n_sp, n_tp, n_groups),
        in_specs=[pl.BlockSpec(memory_space=pltpu.SMEM), ANY_SPEC, VMEM_SPEC, VMEM_SPEC, VMEM_SPEC] + [ANY_SPEC] * 6,
        out_specs=[VMEM_SPEC] * 3,
        out_shape=[jax.ShapeDtypeStruct((n_rows, d_model), BF16), kv_out, kv_out],
        scratch_shapes=[
            pltpu.VMEM((n_rows, d_model), BF16), pltpu.VMEM((q_tiles * d_model, tile), BF16),
            pltpu.VMEM((d_model, head_dim), BF16), pltpu.VMEM((d_model, head_dim), BF16),
            pltpu.VMEM((n_heads * n_rows, head_dim), F32), pltpu.VMEM((n_groups * n_rows, head_dim), F32),
            pltpu.VMEM((n_groups * n_rows, head_dim), F32),
            pltpu.VMEM((SLOTS, HALF * per_row, head_dim), BF16), pltpu.VMEM((SLOTS, HALF * per_row, head_dim), BF16),
            pltpu.VMEM((2, GROUP, n_heads, per_row), F32), pltpu.VMEM((n_rows // HALF,) + half_shape, F32),
            pltpu.VMEM((nx, 2) + half_shape, F32), pltpu.VMEM((nx, 2) + half_shape, F32),
            pltpu.VMEM((2,) + half_shape, F32), pltpu.VMEM((2,) + half_shape, F32), pltpu.VMEM((2,) + half_shape, F32),
            pltpu.VMEM((2, 2 * HALF, n_heads, head_dim), F32), pltpu.VMEM((blk, n_heads * head_dim), BF16),
            pltpu.VMEM((blk, tile), BF16), pltpu.VMEM((n_tp + 1, blk, tile), F32), pltpu.VMEM((2, blk // 2, tile), F32),
            pltpu.VMEM((2, blk // 2, tile), F32), pltpu.VMEM((2, blk // 2, tile), F32),
            pltpu.VMEM((2, n_tp, nx, blk, tile), F32),
            dma((q_tiles + 4,)), dma((2 * SLOTS,)), dma((q_tiles + 2,)), dma((q_tiles + 2,)), dma((8,)), dma((8,)),
            dma((6,)), dma((6,)), dma((7,)), dma((7,)), dma((40,)), dma((40,)), dma((32,)), dma((32,))],
        compiler_params=pltpu.CompilerParams(collective_id=0, has_side_effects=True, vmem_limit_bytes=54 * 2 ** 20),
        name="step",
    )(seq_lens, hidden, vec, cos_t, sin_t, w_q, w_k, w_v, w_o, k_loc, v_loc)


def solution(mesh):
    n_sp, n_tp = mesh.shape['sp'], mesh.shape['tp']

    def device_step(hidden, norm_w, w_q, b_q, w_k, b_k, w_v, b_v, w_o, k_cache, v_cache, positions, seq_lens):
        n_rows = hidden.shape[0]
        groups_dev, head_dim = k_cache.shape[2], k_cache.shape[3]
        rot_dim = head_dim // 2
        lane = jnp.arange(head_dim, dtype=jnp.int32)
        inv_freq = ROPE_BASE ** (-2.0 * (lane // 2).astype(F32) / rot_dim)
        angles = positions.astype(F32)[:, None] * inv_freq
        cos_t = jnp.cos(angles)
        sin_t = jnp.where(lane % 2 == 0, -jnp.sin(angles), jnp.sin(angles))
        vec = jnp.concatenate([norm_w, b_q, b_k, b_v]).astype(F32).reshape(1, -1)
        y_out, k_out, v_out = attention_step(seq_lens, hidden, vec, cos_t, sin_t, w_q, w_k, w_v, w_o,
                                             k_cache.reshape(-1, head_dim), v_cache.reshape(-1, head_dim), n_sp, n_tp, head_dim)
        return y_out, k_out.reshape(n_rows, groups_dev, head_dim), v_out.reshape(n_rows, groups_dev, head_dim)

    col_spec = P(None, 'tp')
    vec_spec = P('tp')
    cache_spec = P('dp', 'sp', 'tp', None)
    group_spec = P('dp', 'tp', None)
    in_specs = (P('dp', None), P(None), col_spec, vec_spec, col_spec, vec_spec, col_spec, vec_spec,
                P('tp', None), cache_spec, cache_spec, P('dp'), P('dp'))
    out_specs = (P('dp', None), group_spec, group_spec)
    return jax.shard_map(device_step, mesh=mesh, in_specs=in_specs, out_specs=out_specs, check_vma=False)
```

time: 161 us -> 81.2 us (0.50)
  Pallas kernels: 144 us -> 68.6 us
  local copies, waits for them, and re-layouts: 11.3 us -> 9.04 us
    pallas_call x3 -> x1, Pallas kernels: 144 us -> 68.6 us  [attention_step(): pl.pallas_call(functools.partial(step_kernel, n_sp, n_tp, n_groups), in_s...]
    unnamed x11 -> x1, local copies, waits for them, and re-layouts: 9.9 us -> 3.13 us
    concatenate x0 -> x4, local copies, waits for them, and re-layouts: none -> 2.73 us  [device_step(): vec = jnp.concatenate([norm_w, b_q, b_k, b_v]).astype(F32).reshape(1, -1)]
    reshape x4 -> x0, other arithmetic: 2.71 us -> none  [the longest x1 0.7 us: qkv_project(): norm_w.astype(F32).reshape(1, d_model)]
where the time goes in v2:
time: 81.2 us; the launch traced here: 80.9 us
  Pallas kernels  68.6 us (84%)
  local copies, waits for them, and re-layouts  9.04 us (11%)
  other arithmetic  2.59 us (3%)
    pallas_call x1, Pallas kernels, attention_step(): pl.pallas_call(functools.partial(step_kernel, n_sp, n_tp, n_groups), in_s...  68.6 us
    unnamed x1, local copies, waits for them, and re-layouts  3.13 us
    concatenate x4, local copies, waits for them, and re-layouts, device_step(): vec = jnp.concatenate([norm_w, b_q, b_k, b_v]).astype(F32).reshape(1, -1)  2.73 us

profile of v2, /device:TPU:97, one launch (start us, length us, event | category | flops | bytes accessed | tf_op | source)
XLA Modules:
  0.0 80.9 jit_solution(17369026950489278477)
XLA Ops:
  0.7 0.7 concatenate.20
  1.3 0.7 concatenate.21
  2.0 0.7 convert_element_type.21
  2.7 0.7 concatenate.19
  3.4 0.7 concatenate.18
  4.1 0.6 maximum_convert_fusion.vec_ref
  4.7 1.2 %negate_select_fusion = (f32[256,128]{1,0:T(8,128)}, f32[256,128]{1,0:T(8,128)}) fusion(f32[128]{0:T(128)S(1)} %fusion.3, f32[256]{0:T(256)S(1)} %convert_element_type.21, pred[128]{0:T(512)(128)(4,1)S(1)} %fusion), kind=kLoop, calls=%fused_computation | loop fusion | flops 98304 | bytes 263808 | tf_op jit(solution)/shard_map/jit(_where)/select_n | solution.py:485
  6.0 68.6 %step.1 = (bf16[256,4096]{1,0:T(8,128)(2,1)}, bf16[256,256]{1,0:T(8,128)(2,1)}, bf16[256,256]{1,0:T(8,128)(2,1)}) custom-call(s32[256]{0:T(256)} %lens_ref.1, bf16[256,4096]{1,0:T(8,128)(2,1)} %hid_ref.1, f32[1,7680]{1,0:T(1,128)} %maximum_convert_fusion.vec_ref, f32[256,128]{1,0:T(8,128)} %get-tuple-element.10.cos_ref, ...), custom_call_target="tpu_custom_call" | custom-call | tf_op jit(solution)/shard_map/step/pallas_call | solution.py:449
  74.6 1.6 %reshape.93 = bf16[256,2,128]{2,1,0:T(2,128)(2,1)} reshape(bf16[256,256]{1,0:T(8,128)(2,1)} %get-tuple-element.7) | data formatting | bytes 262144 | tf_op jit(solution)/shard_map/reshape | solution.py:489
  76.2 1.6 %reshape.94 = bf16[256,2,128]{2,1,0:T(2,128)(2,1)} reshape(bf16[256,256]{1,0:T(8,128)(2,1)} %get-tuple-element.8) | data formatting | bytes 262144 | tf_op jit(solution)/shard_map/reshape | solution.py:489
  77.8 3.1 %copy.17 = bf16[256,4096]{1,0:T(8,128)(2,1)} copy(bf16[256,4096]{1,0:T(8,128)(2,1)} %get-tuple-element.14) | data formatting | bytes 4194304
  (2 shorter events, 0.0 us)
